TPU v7x, 32 devices: a whole 2x2x4 slice. The times are simulated.
32 devices in a mesh: row: 4 (over x, core), col: 8 (over z, y).
Axes of the slice: x: 2, y: 2, z: 4, core: 2. Of those that a mesh axis runs over, the one named last changes fastest.
Arguments:
- hamiltonian: bfloat16 [2912, 2912], P('row', 'col'), may hold values from -6 to 6
- new_atom: int32 [224], replicated, may hold values from 0 to 223, as said below
- pattern: int32 [224, 224], P('row', 'col'), may hold values 0 or 1
Outputs:
- sign_matrix: float32 [2912, 2912], P('row', 'col')
Inputs may be any that keep to these rules, and one draw needn't show every extreme that they name: `new_atom`: each old atom appears once. Block column b holds atoms b * 28 to (b + 1) * 28 - 1 in both orders. For each new block column d and each v from 0 to 27, exactly one atom of new block column d comes from old block column (d - 1 - (v mod 8)) mod 8, so the number of atoms that old block column b sends to new block column (b + k) mod 8 is the number of such v with (1 + v) mod 8 = k.
All inputs are finite; a program needn't handle non-finite values. No bound on the sum of `pattern` on one device may be relied on, other than what follows from the above.
Results may differ from a plain program's by a relative error of at most 0.0029.
Values may be sent and summed in bfloat16 or wider, within the bound.
A program may use at most 64 MiB of HBM per device.

v0:
```python
import functools

import jax
import jax.numpy as jnp
import numpy as np
from jax import lax
from jax.experimental import pallas as pl
from jax.experimental.pallas import tpu as pltpu
from jax.sharding import PartitionSpec as P

NBF = 13
LANE = 128
BF = jnp.bfloat16
F32 = jnp.float32
I32 = jnp.int32
MESH = pl.DeviceIdType.MESH


def up(n, k):
    return -(-n // k) * k


def mm(a, b):
    return jnp.dot(a, b, preferred_element_type=F32)


def mm_nt(a, b):
    return lax.dot_general(a, b, (((1,), (1,)), ((), ())), preferred_element_type=F32)


def spread(rows, lanes, base, count):
    i = lax.broadcasted_iota(I32, (rows, lanes), 0)
    a = lax.broadcasted_iota(I32, (rows, lanes), 1) - base
    hit = (a >= 0) & (a < count) & (i >= a * NBF) & (i < a * NBF + NBF)
    return jnp.where(hit, 1.0, 0.0).astype(BF)


def kernel(
    n_row, n_col, atoms_col, order,
    h_ref, pat_ref, selrow_ref, selcol_ref, slotpos_ref, slotrow_ref, posrow_ref,
    out_ref,
    panel, m, bt, st, ct, bs, pt_in, pt_all, pt_old, tot, tot_all, er,
    own_sem, p1_send, p1_recv, p2_send, p2_recv, t_send, t_recv,
    g_send, g_recv, r_send, r_recv, f_send, b_send, b_recv,
):
    ratio = n_col // n_row
    blk = h_ref.shape[2]
    live = up(atoms_col * NBF, 16)
    av = pat_ref.shape[0]
    outer = n_col // 2
    nx = n_row // 2
    pieces = blk // LANE
    row = lax.axis_index("row")
    col = lax.axis_index("col")
    hi, lo = col // 2, col % 2
    x, core = row // 2, row % 2
    peer_row = x * 2 + 1 - core

    def chunk_piece(c, t):
        return panel.at[c, t, pl.ds(0, live), :]

    own = []
    for t in range(ratio):
        cp = pltpu.make_async_copy(h_ref.at[t, pl.ds(0, live), :], chunk_piece(col, t), own_sem.at[t])
        cp.start()
        own.append(cp)

    barrier = pltpu.get_barrier_semaphore()
    for k in range(1, n_row):
        pl.semaphore_signal(barrier, inc=1, device_id={"row": (row + k) % n_row, "col": col}, device_id_type=MESH)
    for k in range(1, n_col):
        pl.semaphore_signal(barrier, inc=1, device_id={"row": row, "col": (col + k) % n_col}, device_id_type=MESH)
    pl.semaphore_wait(barrier, n_row + n_col - 2)

    def hop(c, t, way):
        to = [col + 2, col - 2, hi * 2 + 1 - lo][way]
        return pltpu.make_async_remote_copy(
            src_ref=chunk_piece(c, t), dst_ref=chunk_piece(c, t),
            send_sem=g_send.at[way, c, t], recv_sem=g_recv.at[c, t],
            device_id={"row": row, "col": to}, device_id_type=MESH,
        )

    for t in range(ratio):
        own[t].wait()

        @pl.when(hi + 1 < outer)
        def _():
            hop(col, t, 0).start()

        @pl.when(hi > 0)
        def _():
            hop(col, t, 1).start()

        hop(col, t, 2).start()

    def p1(k):
        return pltpu.make_async_remote_copy(
            src_ref=pat_ref, dst_ref=pt_in.at[row], send_sem=p1_send.at[k], recv_sem=p1_recv.at[row],
            device_id={"row": (row + k) % n_row, "col": col}, device_id_type=MESH,
        )

    def p2(k):
        return pltpu.make_async_remote_copy(
            src_ref=pt_all.at[col], dst_ref=pt_all.at[col], send_sem=p2_send.at[k], recv_sem=p2_recv.at[col],
            device_id={"row": row, "col": (col + k) % n_col}, device_id_type=MESH,
        )

    for k in range(1, n_row):
        p1(k).start()
    panel[:, :, live:, :] = jnp.zeros((n_col, ratio, blk - live, blk), BF)
    for t in range(ratio):
        er[t * blk : (t + 1) * blk, :] = spread(blk, LANE, t * atoms_col, atoms_col)
    ec = spread(blk, av, 0, atoms_col)
    pt_in[row] = pat_ref[...]
    tot[...] = jnp.zeros_like(tot)
    for k in range(1, n_row):
        src = (row + k) % n_row
        pltpu.make_async_copy(pt_in.at[src], pt_in.at[src], p1_recv.at[src]).wait()
    old_rows = jnp.zeros((av, LANE), F32)
    for r in range(n_row):
        old_rows += mm(pt_in[r], selrow_ref[r])
    pt_all[col] = old_rows.astype(BF)
    for k in range(1, n_col):
        p2(k).start()
    for k in range(1, n_col):
        src = (col + k) % n_col
        pltpu.make_async_copy(pt_all.at[src], pt_all.at[src], p2_recv.at[src]).wait()
    everything = pt_all[...].reshape(n_col * av, LANE)
    for c in range(n_col):
        pt_old[c] = mm(selcol_ref[c], everything).astype(BF)

    def arrived(c, t):
        pltpu.make_async_copy(chunk_piece(c, t), chunk_piece(c, t), g_recv.at[c, t]).wait()

    def b_copy(c, k):
        return pltpu.make_async_remote_copy(
            src_ref=bs.at[row, c], dst_ref=bs.at[row, c], send_sem=b_send.at[k, c], recv_sem=b_recv.at[row, c],
            device_id={"row": (row + k) % n_row, "col": col}, device_id_type=MESH,
        )

    def process(c):
        mask_rows = mm_nt(er[...], pt_old[c]).astype(BF)
        keep = mm_nt(mask_rows, ec)
        j = lax.broadcasted_iota(I32, (slotpos_ref.shape[1], blk), 1)
        pick = jnp.where(slotpos_ref[c] == j + c * blk, 1.0, 0.0).astype(BF)
        for t in range(ratio):
            part = jnp.where(keep[t * blk : (t + 1) * blk] > 0.5, panel[c, t].astype(F32), 0.0)
            tot[...] += jnp.sum((part * part).reshape(blk // 8, 8, blk), axis=0)
            part = part.astype(BF)
            m[c, t * blk : (t + 1) * blk, :] = part
            bs[row, c, :, t * blk : (t + 1) * blk] = mm_nt(pick, part).astype(BF)
        for k in range(1, n_row):
            b_copy(c, k).start()

    def step(d, _):
        for way in range(2):
            src = hi - d if way == 0 else hi + d
            ok = (d > 0) & (d < outer) & (src >= 0) & (src < outer)

            @pl.when(ok)
            def _():
                c = src * 2 + lo
                more = hi + 1 < outer if way == 0 else hi > 0
                for t in range(ratio):
                    arrived(c, t)

                    @pl.when(more)
                    def _():
                        hop(c, t, way).start()

                    hop(c, t, 2).start()

        def candidate(k, _):
            kind, way = k // 2, k % 2
            dist = d - kind
            src = hi + (1 - 2 * way) * dist
            ok = (dist >= 0) & (dist < outer) & (src >= 0) & (src < outer) & ((dist > 0) | (way == 0))

            @pl.when(ok)
            def _():
                c = src * 2 + jnp.where(kind == 0, lo, 1 - lo)

                @pl.when(kind == 1)
                def _():
                    for t in range(ratio):
                        arrived(c, t)

                process(c)

            return 0

        lax.fori_loop(0, 4, candidate, 0)
        return 0

    lax.fori_loop(0, outer + 1, step, 0)

    def share(buf, stage, p):
        def part(r):
            return buf.at[r, pl.ds(p * LANE, LANE), :]

        def send(r, to, sem):
            return pltpu.make_async_remote_copy(
                src_ref=part(r), dst_ref=part(r), send_sem=sem, recv_sem=r_recv.at[stage, p, r],
                device_id={"row": to, "col": col}, device_id_type=MESH,
            )

        return (
            [send(row, (x + k) % nx * 2 + core, r_send.at[stage, p, k]) for k in range(1, nx)]
            + [send(row, peer_row, r_send.at[stage, p, 0])],
            [send((x + k) % nx * 2 + core, peer_row, f_send.at[stage, p, k]) for k in range(1, nx)],
        )

    def start_own(buf, stage, p):
        for cp in share(buf, stage, p)[0]:
            cp.start()

    def got(buf, stage, p, r):
        ref = buf.at[r, pl.ds(p * LANE, LANE), :]
        pltpu.make_async_copy(ref, ref, r_recv.at[stage, p, r]).wait()

    def relay(buf, stage, p):
        onward = share(buf, stage, p)[1]
        for k in range(1, nx):
            got(buf, stage, p, (x + k) % nx * 2 + core)
            onward[k - 1].start()

    def finish(buf, stage, p):
        for k in range(nx):
            got(buf, stage, p, (x + k) % nx * 2 + 1 - core)

    def drain(buf, stage, p):
        first, onward = share(buf, stage, p)
        for cp in first + onward:
            cp.wait_send()

    def t_copy(k):
        return pltpu.make_async_remote_copy(
            src_ref=tot_all.at[row], dst_ref=tot_all.at[row], send_sem=t_send.at[k], recv_sem=t_recv.at[row],
            device_id={"row": (row + k) % n_row, "col": col}, device_id_type=MESH,
        )

    part_sum = tot[:, 0:LANE]
    for q in range(1, pieces):
        part_sum += tot[:, q * LANE : (q + 1) * LANE]
    tot_all[row] = part_sum
    for k in range(1, n_row):
        t_copy(k).start()
    for k in range(1, n_row):
        src = (row + k) % n_row
        pltpu.make_async_copy(tot_all.at[src], tot_all.at[src], t_recv.at[src]).wait()
    total = jnp.sum(jnp.sum(tot_all[...], axis=0), axis=(0, 1), keepdims=True)
    s = lax.rsqrt(total / order)

    def panel_product(buf, p):
        result = jnp.zeros((LANE, ratio * blk), F32)
        for c in range(n_col):
            t = c % ratio
            result += mm_nt(buf[c // ratio, p * LANE : (p + 1) * LANE, t * blk : (t + 1) * blk], m[c])
        return result

    mask_cols = mm(ec, pt_all[col]).astype(BF)
    slots = n_col * slotpos_ref.shape[1]
    q = lax.broadcasted_iota(I32, (blk, slots), 1)
    compact = jnp.where(slotrow_ref[...] == q, 1.0, 0.0).astype(BF)
    bt[row] = mm(compact, bs[row].reshape(slots, ratio * blk)).astype(BF)
    for k in range(1, n_row):
        src = (row + k) % n_row

        def b_got(c, _):
            pltpu.make_async_copy(bs.at[src, c], bs.at[src, c], b_recv.at[src, c]).wait()
            return 0

        lax.fori_loop(0, n_col, b_got, 0)
        bt[src] = mm(compact, bs[src].reshape(slots, ratio * blk)).astype(BF)
    for p in range(pieces):
        keep = mm_nt(mask_cols[p * LANE : (p + 1) * LANE], er[...])
        square = panel_product(bt, p) * (s * s)
        st[row, p * LANE : (p + 1) * LANE, :] = jnp.where(keep > 0.5, square, 0.0).astype(BF)
        start_own(st, 1, p)

    def pick_rows(r):
        j = lax.broadcasted_iota(I32, (ratio * blk, ratio * blk), 1)
        return jnp.where(posrow_ref[...] == j + r * (ratio * blk), 1.0, 0.0).astype(BF)

    start = jnp.zeros((ratio * blk, blk), F32)
    for r in range(n_row):
        start += mm_nt(pick_rows(r), bt[r])
    start = 1.5 * (start * s).astype(BF).astype(F32)
    for t in range(ratio):
        out_ref[t] = start[t * blk : (t + 1) * blk]
    for p in range(pieces):
        relay(st, 1, p)
        finish(st, 1, p)
        cube = panel_product(st, p) * s
        ct[row, p * LANE : (p + 1) * LANE, :] = cube.astype(BF)
        start_own(ct, 2, p)
    for p in range(pieces):
        relay(ct, 2, p)
    for p in range(pieces):
        finish(ct, 2, p)
    mine = mm_nt(er[...], pat_ref[...]).astype(BF)
    keep = mm_nt(mine, ec)
    cube = jnp.zeros((ratio * blk, blk), F32)
    for r in range(n_row):
        cube += mm_nt(pick_rows(r), ct[r])
    for t in range(ratio):
        part = slice(t * blk, (t + 1) * blk)
        out_ref[t] = jnp.where(keep[part] > 0.5, out_ref[t] - 0.5 * cube[part], 0.0)

    for k in range(1, n_row):
        p1(k).wait_send()
        t_copy(k).wait_send()
    for k in range(1, n_col):
        p2(k).wait_send()

    def sent(q, _):
        c = q * 2 + lo
        for t in range(ratio):

            @pl.when((q <= hi) & (hi + 1 < outer))
            def _():
                hop(c, t, 0).wait_send()

            @pl.when((q >= hi) & (hi > 0))
            def _():
                hop(c, t, 1).wait_send()

            hop(c, t, 2).wait_send()
        return 0

    lax.fori_loop(0, outer, sent, 0)
    def b_sent(c, _):
        for k in range(1, n_row):
            b_copy(c, k).wait_send()
        return 0

    lax.fori_loop(0, n_col, b_sent, 0)
    for stage, buf in ((1, st), (2, ct)):
        for p in range(pieces):
            drain(buf, stage, p)


def on_device(hamiltonian, new_atom, pattern):
    rows_here, cols_here = hamiltonian.shape
    n_row, n_col = lax.axis_size("row"), lax.axis_size("col")
    ratio = n_col // n_row
    ar, ac = pattern.shape
    order = rows_here * n_row
    blk = up(cols_here, LANE)
    av = up(ac, 16)
    row_here = lax.axis_index("row")
    col_here = lax.axis_index("col")
    pad = blk - cols_here
    h = jnp.pad(hamiltonian.reshape(ratio, cols_here, cols_here), ((0, 0), (0, pad), (0, pad)))
    pat_t = jnp.pad(pattern.astype(BF).T, ((0, av - ac), (0, LANE - ar)))
    by_row = jnp.pad(new_atom.reshape(n_row, ar), ((0, 0), (0, LANE - ar)), constant_values=-1)
    i = jnp.arange(LANE, dtype=I32)
    selrow = ((by_row[:, :, None] == row_here * ar + i) & (i < ar)).astype(BF)
    by_col = jnp.pad(new_atom.reshape(n_col, ac), ((0, 0), (0, av - ac)), constant_values=-1).reshape(-1)
    v = jnp.arange(av, dtype=I32)
    old = jnp.arange(n_col, dtype=I32)[:, None] * ac + v[None, :]
    selcol = ((by_col[None, None, :] == old[:, :, None]) & (v < ac)[None, :, None]).astype(BF)
    place = new_atom // ac * blk + new_atom % ac * NBF

    def positions(here):
        mine = lax.dynamic_slice_in_dim(place, here * ac, ac)
        q = jnp.arange(blk, dtype=I32)
        a = jnp.arange(ac, dtype=I32)
        hit = (q[:, None] >= a * NBF) & (q[:, None] < a * NBF + NBF)
        base = jnp.sum(jnp.where(hit, (mine - a * NBF)[None, :], 0), axis=1)
        return jnp.where(q < ac * NBF, base + q, -1)

    poscol = positions(col_here)
    most = int(np.max(np.bincount((1 + np.arange(ac)) % n_col, minlength=n_col)))
    sl = up(most * NBF, 16)
    source = lax.dynamic_slice_in_dim(new_atom, col_here * ac, ac) // ac
    a = jnp.arange(ac, dtype=I32)
    rank = jnp.sum(((source[:, None] == source[None, :]) & (a[None, :] < a[:, None])).astype(I32), axis=1)
    q = jnp.arange(blk, dtype=I32)
    hit = (q[:, None] >= a * NBF) & (q[:, None] < a * NBF + NBF)
    base = jnp.sum(jnp.where(hit, (source * sl + rank * NBF - a * NBF)[None, :], 0), axis=1)
    slotrow = jnp.where(q < ac * NBF, base + q, -1)
    slotpos = jnp.sum(jnp.where(jnp.arange(n_col * sl, dtype=I32)[:, None] == slotrow[None, :], poscol[None, :] + 1, 0), axis=1) - 1
    slotpos = slotpos.reshape(n_col, sl, 1)
    slotrow = slotrow[:, None]
    posrow = jnp.concatenate([positions(row_here * ratio + t) for t in range(ratio)])[:, None]
    pieces = blk // LANE
    vm = pl.BlockSpec(memory_space=pltpu.VMEM)
    dma = pltpu.SemaphoreType.DMA
    wide = ratio * blk
    out = pl.pallas_call(
        functools.partial(kernel, n_row, n_col, ac, float(order)),
        out_shape=jax.ShapeDtypeStruct((ratio, blk, blk), F32),
        in_specs=[pl.BlockSpec(memory_space=pl.ANY)] + [vm] * 6,
        out_specs=vm,
        scratch_shapes=[
            pltpu.VMEM((n_col, ratio, blk, blk), BF),
            pltpu.VMEM((n_col, wide, blk), BF),
            pltpu.VMEM((n_row, blk, wide), BF),
            pltpu.VMEM((n_row, blk, wide), BF),
            pltpu.VMEM((n_row, blk, wide), BF),
            pltpu.VMEM((n_row, n_col, sl, wide), BF),
            pltpu.VMEM((n_row, av, LANE), BF),
            pltpu.VMEM((n_col, av, LANE), BF),
            pltpu.VMEM((n_col, av, LANE), BF),
            pltpu.VMEM((8, blk), F32),
            pltpu.VMEM((n_row, 8, LANE), F32),
            pltpu.VMEM((wide, LANE), BF),
            dma((ratio,)),
            dma((n_row,)),
            dma((n_row,)),
            dma((n_col,)),
            dma((n_col,)),
            dma((n_row,)),
            dma((n_row,)),
            dma((3, n_col, ratio)),
            dma((n_col, ratio)),
            dma((3, pieces, n_row)),
            dma((3, pieces, n_row)),
            dma((3, pieces, n_row)),
            dma((n_row, n_col)),
            dma((n_row, n_col)),
        ],
        compiler_params=pltpu.CompilerParams(
            collective_id=0, has_side_effects=True, vmem_limit_bytes=60 * 1024 * 1024
        ),
    )(h, pat_t, selrow, selcol, slotpos, slotrow, posrow)
    return out[:, :cols_here, :cols_here].reshape(rows_here, cols_here)


def solution(mesh):
    in_specs = (P("row", "col"), P(), P("row", "col"))
    out_specs = P("row", "col")
    return jax.shard_map(
        on_device, mesh=mesh, in_specs=in_specs, out_specs=out_specs, check_vma=False
    )
```

profile of v0, /device:TPU:0, one launch (start us, length us, event | category | flops | bytes accessed | tf_op | source)
XLA Modules:
  0.0 120.4 jit_solution(11488598894907086229)
XLA Ops:
  0.0 0.0 copy-start
  0.0 0.8 fusion.4
  0.8 0.8 dynamic-slice_subtract_fusion
  1.6 0.2 convert_reduce_fusion
  1.8 0.8 reshape.118
  2.5 0.1 iota_add_fusion
  2.6 0.8 reshape.119
  3.4 0.1 eq.59
  3.4 0.1 select_reduce_fusion.2
  3.6 0.2 select_reduce_fusion
  3.8 0.7 convert_bitcast_fusion
  4.5 0.6 pad.17.pat_ref
  5.1 0.8 and_convert_fusion.selcol_ref
  5.9 0.8 and_convert_fusion.1.selrow_ref
  6.7 0.8 fusion.slotrow_ref
  7.5 0.9 sub.36.slotpos_ref
  8.4 0.9 broadcast_in_dim.99.posrow_ref
  9.3 0.0 copy-done
  9.3 0.1 reshape.117
  9.4 0.9 pad.16.h_ref
  10.3 107.6 %shard_map.37 = f32[2,384,384]{2,1,0:T(8,128)} custom-call(bf16[2,384,384]{2,1,0:T(8,128)(2,1)} %pad.16.h_ref, bf16[32,128]{1,0:T(8,128)(2,1)} %pad.17.pat_ref, bf16[4,128,128]{2,1,0:T(8,128)(2,1)} %and_convert_fusion.1.selrow_ref, bf16[8,32,256]{2,1,0:T(8,128)(2,1)} %and_convert_fusion.selcol_ref, s32[8,64,1]{2,1,0:T(8,128)} %sub.36.slotpos_ref, ...), custom_call_target="tpu_custom_call" | custom-call | tf_op jit(solution)/shard_map/pallas_call | solution.py:391
  118.0 1.3 %slice.3 = f32[2,364,364]{2,1,0:T(8,128)S(1)} slice(f32[2,384,384]{2,1,0:T(8,128)} %shard_map.37), slice={[0:2], [0:364], [0:364]} | slice | bytes 2119936 | tf_op jit(solution)/shard_map/slice | solution.py:428
  119.3 1.1 reshape.120
  (14 shorter events, 0.1 us)
Async XLA Ops:
  0.0 9.3 %copy-start = (bf16[728,364]{1,0:T(8,128)(2,1)S(1)}, bf16[728,364]{1,0:T(8,128)(2,1)}, u32[]{:S(2)}) copy-start(bf16[728,364]{1,0:T(8,128)(2,1)} %param.3) | copy-start | bytes 1589956
where the time goes:
time: 121 us; the launch traced here: 120 us
  Pallas kernels  108 us (89%)
  local copies, waits for them, and re-layouts  7.49 us (6%)
  other arithmetic  5.2 us (4%)
    pallas_call x1, Pallas kernels, on_device(): pl.pallas_call(functools.partial(kernel, n_row, n_col, ac, float(order)),...  108 us

commit v1 on v0

v1 whole, which is shorter than its diff:
```python
import functools

import jax
import jax.numpy as jnp
import numpy as np
from jax import lax
from jax.experimental import pallas as pl
from jax.experimental.pallas import tpu as pltpu
from jax.sharding import PartitionSpec as P

NBF = 13
LANE = 128
BF = jnp.bfloat16
F32 = jnp.float32
I32 = jnp.int32
MESH = pl.DeviceIdType.MESH
FAR = -1.0e6


def up(n, k):
    return -(-n // k) * k


def mm(a, b):
    return jnp.dot(a, b, preferred_element_type=F32)


def mm_nt(a, b):
    return lax.dot_general(a, b, (((1,), (1,)), ((), ())), preferred_element_type=F32)


def iota(shape, axis):
    return lax.broadcasted_iota(I32, shape, axis)


def fiota(shape, axis):
    return iota(shape, axis).astype(F32)


def whole_part(x, n):
    return jnp.floor((x + 0.5) * (1.0 / n))


def expand(sel, lo, start, size):
    u = fiota((lo.shape[0], size), 1) - lo
    hit = sel & (u >= 0.0) & (u < NBF)
    return jnp.sum(jnp.where(hit, u + (start + 1.0), 0.0), axis=0, keepdims=True) - 1.0


def onehot(rows, places, offset=0):
    i = fiota((rows, places.shape[1]), 0) + float(offset)
    return jnp.where(i == places, 1.0, 0.0).astype(BF)


class Plan:
    def __init__(self, n_row, n_col, rows, cols, ar, ac):
        self.n_row, self.n_col, self.rows, self.cols, self.ar, self.ac = n_row, n_col, rows, cols, ar, ac
        self.ratio = n_col // n_row
        self.nx = n_row // 2
        self.outer = n_col // 2
        self.av = up(ac, 16)
        self.w = n_col * self.av
        self.blk = up(cols, LANE)
        self.live = up(rows, 16)
        self.wide = up(rows, LANE)
        count = np.bincount((1 + np.arange(ac)) % n_col, minlength=n_col)
        self.slot = up(int(count.max()) * NBF, 16)
        r = self.ratio
        pair = [
            sum(int(count[(r * k + g - b) % n_col]) for b in range(r) for g in range(r)) for k in range(n_row)
        ]
        self.sl = up(max(pair) * NBF, 16)
        self.slp = up(self.sl, LANE)
        own = pair[0] * NBF // 16 * 16
        chip = (pair[0] + min(pair[1], pair[n_row - 1])) * NBF // 16 * 16
        rest = self.live - chip
        last = up(rest // 4, 16)
        ends = [0, own, chip, self.live - last, self.live]
        self.starts, self.sizes = ends[:-1], [b - a for a, b in zip(ends, ends[1:])]
        self.joff = [(0, self.blk - LANE), (self.blk - LANE, LANE)]


def kernel(
    s_, order, h_ref, na_ref, pat_ref, out_ref,
    hv, hp, xs, rin, pp, pt_all, mr, kq, panel, left, racc, rt, rx, xm, fm, sta, stb, cac, tot, tot_all,
    h_sem, x_send, x_recv, p_send, p_recv, t_send, t_recv, g_send, g_recv, r_send, r_recv, f_send,
):
    n_row, n_col, ratio, nx, outer = s_.n_row, s_.n_col, s_.ratio, s_.nx, s_.outer
    ac, ar, av, W, blk, live, wide = s_.ac, s_.ar, s_.av, s_.w, s_.blk, s_.live, s_.wide
    slot, sl, slp = s_.slot, s_.sl, s_.slp
    row = lax.axis_index("row")
    col = lax.axis_index("col")
    hi, lo = col // 2, col % 2
    x, core = row // 2, row % 2
    peer = x * 2 + 1 - core
    n_piece = len(s_.sizes)
    slots = n_col * slot

    h_copy = pltpu.make_async_copy(h_ref, hv, h_sem.at[0])
    h_copy.start()
    barrier = pltpu.get_barrier_semaphore()
    for k in range(1, n_row):
        pl.semaphore_signal(barrier, inc=1, device_id={"row": (row + k) % n_row, "col": col}, device_id_type=MESH)
    for k in range(1, n_col):
        pl.semaphore_signal(barrier, inc=1, device_id={"row": row, "col": (col + k) % n_col}, device_id_type=MESH)

    rowf, colf, xf, coref, peerf = [i.astype(F32) for i in (row, col, x, core, peer)]

    def places(w):
        d = whole_part(w, av)
        v = w - d * av
        return d, v, v < ac

    def source(na, d):
        b = whole_part(na, ac)
        src = whole_part(b, ratio)
        home = whole_part(d, ratio)
        far = jnp.where(whole_part(src, 2) == whole_part(home, 2), 1.0, 2.0)
        return b, src, home, jnp.where(src == home, 0.0, far)

    wc, wr = fiota((W, 1), 0), fiota((1, W), 1)
    dc, vc, okc = places(wc)
    dr, vr, okr = places(wr)
    atoms = na_ref[...].astype(F32)
    here = (fiota((W, atoms.shape[1]), 1) == dc * ac + vc) & okc
    nac = jnp.sum(jnp.where(here, atoms, 0.0), axis=1, keepdims=True)
    nar = jnp.sum(jnp.where(fiota((W, W), 0) == wr, nac, 0.0), axis=0, keepdims=True)
    bc, srcc, homec, grpc = source(nac, dc)
    br, srcr, homer, grpr = source(nar, dr)
    before = wr < wc

    def rank(hit):
        return jnp.sum(jnp.where(hit & okr, 1.0, 0.0), axis=1, keepdims=True)

    rank_slot = rank((dr == dc) & (br == bc) & before)
    rank_pair = rank((homer == homec) & (srcr == srcc) & before)
    rank_all = rank((homer == homec) & ((grpr < grpc) | ((grpr == grpc) & before)))
    old_at = NBF * (nac - srcc * ar)
    kx = whole_part(homec, 2) - xf
    kx = jnp.where(kx < 0.0, kx + nx, kx)
    kc = homec - 2.0 * whole_part(homec, 2)
    kc = jnp.where(kc == coref, 0.0, 1.0)
    from_me = okc & (srcc == rowf)
    to_me = okc & (homec == rowf)
    out_place = expand(from_me, old_at, (2.0 * kx + kc) * slp + NBF * rank_pair, wide)
    own_place = expand(from_me & to_me, old_at, NBF * rank_all, wide)

    def other(sign, k):
        return ((x + sign * (k // 2) + nx) % nx) * 2 + (core + k % 2) % 2

    in_place = {
        k: expand(to_me & (srcc == other(-1, k).astype(F32)), NBF * rank_pair, NBF * rank_all, slp)
        for k in range(1, n_row)
    }

    pp[...] = jnp.zeros_like(pp)
    pp[0:ar, 0:ac] = pat_ref[...].astype(F32).astype(BF)
    flip = jnp.where(iota((av, LANE), 0) == iota((av, LANE), 1), 1.0, 0.0).astype(BF)
    pt_all[col] = mm_nt(flip, pp[...]).astype(BF)
    hp[...] = jnp.zeros_like(hp)
    rin[:, sl:, :] = jnp.zeros((n_row - 1, slp - sl, blk), BF)
    rt[:, live:, :] = jnp.zeros((n_row, wide - live, blk), BF)
    sta[:, live:, :] = jnp.zeros((n_row, wide - live, sta.shape[2]), BF)
    stb[:, live:, :] = jnp.zeros((n_row, wide - live, stb.shape[2]), BF)
    tot[...] = jnp.zeros_like(tot)
    racc[...] = jnp.zeros_like(racc)
    h_copy.wait()
    hp[0 : s_.rows, 0 : s_.cols] = hv[...]

    def pick(k):
        xs[k - 1] = mm(onehot(sl, out_place, k * slp), hp[...]).astype(BF)

    def piece(c, p):
        return panel.at[c, pl.ds(s_.starts[p], s_.sizes[p]), :]

    def assemble(p):
        i0, n = s_.starts[p], s_.sizes[p]
        part = None
        if p < 2:
            part = mm(onehot(n, own_place, i0), hp[...])
        for k in range(1, n_row):
            if p >= (1 if k == 1 else 2):
                more = mm(onehot(n, in_place[k], i0), rin[k - 1])
                part = more if part is None else part + more
        panel[col, i0 : i0 + n, :] = part.astype(BF)

    pl.semaphore_wait(barrier, n_row + n_col - 2)

    def x_copy(k):
        return pltpu.make_async_remote_copy(
            src_ref=xs.at[k - 1], dst_ref=rin.at[k - 1, pl.ds(0, sl), :],
            send_sem=x_send.at[k], recv_sem=x_recv.at[k],
            device_id={"row": other(1, k), "col": col}, device_id_type=MESH,
        )

    def p_copy(k):
        return pltpu.make_async_remote_copy(
            src_ref=pt_all.at[col], dst_ref=pt_all.at[col], send_sem=p_send.at[k], recv_sem=p_recv.at[col],
            device_id={"row": row, "col": (col + k) % n_col}, device_id_type=MESH,
        )

    def hop(c, p, way):
        to = [col + 2, col - 2, hi * 2 + 1 - lo][way]
        return pltpu.make_async_remote_copy(
            src_ref=piece(c, p), dst_ref=piece(c, p),
            send_sem=g_send.at[way, c, p], recv_sem=g_recv.at[c, p],
            device_id={"row": row, "col": to}, device_id_type=MESH,
        )

    def by_line(at, src, p):
        inner = ((at == 1) & (src == 0)) | ((at == outer - 2) & (src == outer - 1))
        edge = ((at == outer - 1) & (src == outer - 2)) | ((at == 0) & (src == 1))
        return (inner | edge) if p % 2 == 0 else inner

    def start_own_piece(p):
        @pl.when(hi + 1 < outer)
        def _():
            hop(col, p, 0).start()

        @pl.when(hi > 0)
        def _():
            hop(col, p, 1).start()

        hop(col, p, 2).start()

    for k in range(1, n_col):
        p_copy(k).start()
    assemble(0)
    start_own_piece(0)
    for k in [*range(2, n_row), 1]:
        pick(k)
        x_copy(k).start()

    er_at = fiota((1, LANE), 1)
    er_d = whole_part(er_at, ac)
    er_w = (rowf * ratio + er_d) * av + er_at - er_d * ac
    first = jnp.sum(jnp.where((wc == er_w) & (er_at < ar), NBF * rank_all + 1.0e6, 0.0), axis=0, keepdims=True) - 1.0e6
    u = fiota((live, LANE), 0) - first
    er = jnp.where((u >= 0.0) & (u < NBF), 1.0, 0.0).astype(BF)

    x_copy(1).wait_recv()
    assemble(1)
    start_own_piece(1)
    for k in range(1, n_col):
        src = (col + k) % n_col
        pltpu.make_async_copy(pt_all.at[src], pt_all.at[src], p_recv.at[src]).wait()
    mr[...] = mm_nt(er, pt_all[...].reshape(W, LANE)).astype(BF)

    slot_at = dc * slot + NBF * rank_slot
    mine = okc & (dc == colf)

    def process(c, p):
        i0, n = s_.starts[p], s_.sizes[p]
        lo_c = NBF * (nac - c.astype(F32) * ac)
        t = fiota((W, blk), 1) - lo_c
        hit = (t >= 0.0) & (t < NBF) & okc
        keep = mm(mr[i0 : i0 + n, :], jnp.where(hit, 1.0, 0.0).astype(BF))
        part = jnp.where(keep > 0.5, panel[c, i0 : i0 + n, :].astype(F32), 0.0)
        tot[...] += jnp.sum((part * part).reshape(n // 8, 8, blk), axis=0)
        part = part.astype(BF)
        to_slot = jnp.sum(jnp.where(hit, t + (slot_at + 1.0), 0.0), axis=0, keepdims=True) - 1.0
        to_new = jnp.sum(jnp.where(hit & mine, t + (NBF * vc + 1.0), 0.0), axis=0, keepdims=True) - 1.0
        left[c, i0 : i0 + n, :] = mm_nt(part, onehot(slots, to_slot)).astype(BF)
        racc[i0 : i0 + n, :] += mm_nt(part, onehot(blk, to_new))

    def arrived(c, p):
        pltpu.make_async_copy(piece(c, p), piece(c, p), g_recv.at[c, p]).wait()

    def gather(p):
        def step(d, _):
            for way in range(2):
                src = hi - d if way == 0 else hi + d
                ok = (d > 0) & (d < outer) & (src >= 0) & (src < outer)

                @pl.when(ok)
                def _():
                    c = src * 2 + lo
                    arrived(c, p)

                    @pl.when(hi + 1 < outer if way == 0 else hi > 0)
                    def _():
                        hop(c, p, way).start()

                    @pl.when(jnp.logical_not(by_line(hi, src, p)))
                    def _():
                        hop(c, p, 2).start()

            @pl.when(d == 1)
            def _():
                c = hi * 2 + 1 - lo
                arrived(c, p)

                @pl.when((hi + 1 < outer) & by_line(hi + 1, hi, p))
                def _():
                    hop(c, p, 0).start()

                @pl.when((hi > 0) & by_line(hi - 1, hi, p))
                def _():
                    hop(c, p, 1).start()

            def candidate(k, _):
                kind, way = k // 2, k % 2
                dist = d - kind
                src = hi + (1 - 2 * way) * dist
                ok = (dist >= 0) & (dist < outer) & (src >= 0) & (src < outer) & ((dist > 0) | (way == 0))

                @pl.when(ok)
                def _():
                    c = src * 2 + jnp.where(kind == 0, lo, 1 - lo)

                    @pl.when((kind == 1) & (dist > 0))
                    def _():
                        arrived(c, p)

                    process(c, p)

                return 0

            lax.fori_loop(0, 4, candidate, 0)
            return 0

        lax.fori_loop(0, outer + 1, step, 0)

    def part_of(r, ix):
        if ix < n_piece:
            return rt.at[r, pl.ds(s_.starts[ix], s_.sizes[ix]), :]
        return (sta, stb)[ix - n_piece].at[r, pl.ds(0, live), :]

    def share(ix):
        def send(r, to, sem):
            return pltpu.make_async_remote_copy(
                src_ref=part_of(r, ix), dst_ref=part_of(r, ix), send_sem=sem, recv_sem=r_recv.at[ix, r],
                device_id={"row": to, "col": col}, device_id_type=MESH,
            )

        return (
            [send(row, (x + k) % nx * 2 + core, r_send.at[ix, k]) for k in range(1, nx)]
            + [send(row, peer, r_send.at[ix, 0])],
            [send((x + k) % nx * 2 + core, peer, f_send.at[ix, k]) for k in range(1, nx)],
        )

    def start_share(ix):
        for cp in share(ix)[0]:
            cp.start()

    def got(ix, r):
        pltpu.make_async_copy(part_of(r, ix), part_of(r, ix), r_recv.at[ix, r]).wait()

    def relay(ix):
        onward = share(ix)[1]
        for k in range(1, nx):
            got(ix, (x + k) % nx * 2 + core)
            onward[k - 1].start()

    def finish(ix):
        for k in range(nx):
            got(ix, (x + k) % nx * 2 + 1 - core)

    def right_piece(p):
        i0, n = s_.starts[p], s_.sizes[p]
        rt[row, i0 : i0 + n, :] = racc[i0 : i0 + n, :].astype(BF)
        start_share(p)

    gather(0)
    for k in range(2, n_row):
        x_copy(k).wait_recv()
    for p in range(2, n_piece):
        assemble(p)
        start_own_piece(p)
    right_piece(0)
    gather(1)
    right_piece(1)
    relay(0)
    for r in range(n_row):
        ws = slice(r * ratio * av, (r + 1) * ratio * av)
        at = (dc[ws] - float(r * ratio)) * slots + bc[ws] * slot + NBF * rank_slot[ws]
        xm[r] = onehot(ratio * slots, expand(okc[ws], NBF * rank_all[ws], at, wide))
    my_new = NBF * ((dc - rowf * ratio) * ac + vc)
    fm[...] = onehot(s_.rows, expand(to_me, NBF * rank_all, my_new, wide))
    t = fiota((W, blk), 1) - NBF * vc
    kq[...] = mm(mr[...], jnp.where((t >= 0.0) & (t < NBF) & mine, 1.0, 0.0).astype(BF)).astype(BF)
    gather(2)
    right_piece(2)
    relay(1)
    gather(3)
    right_piece(3)

    def t_copy(k):
        return pltpu.make_async_remote_copy(
            src_ref=tot_all.at[row], dst_ref=tot_all.at[row], send_sem=t_send.at[k], recv_sem=t_recv.at[row],
            device_id={"row": (row + k) % n_row, "col": col}, device_id_type=MESH,
        )

    part_sum = tot[:, 0:LANE]
    for q in range(1, blk // LANE):
        part_sum += tot[:, q * LANE : (q + 1) * LANE]
    tot_all[row] = part_sum
    for k in range(1, n_row):
        t_copy(k).start()
    relay(2)
    for p in range(3):
        finish(p)
    relay(3)
    finish(3)
    for r in range(n_row):
        rx[r] = mm(xm[r], rt[r]).astype(BF)
    for k in range(1, n_row):
        src = (row + k) % n_row
        pltpu.make_async_copy(tot_all.at[src], tot_all.at[src], t_recv.at[src]).wait()
    total = jnp.sum(jnp.sum(tot_all[...], axis=0), axis=(0, 1), keepdims=True)
    scale = lax.rsqrt(total / order)
    half = live // 2

    def product(i0, j0, width):
        acc = None
        for c in range(n_col):
            b = jnp.concatenate(
                [
                    rx[d // ratio, (d % ratio) * slots + c * slot : (d % ratio) * slots + (c + 1) * slot, j0 : j0 + width]
                    for d in range(n_col)
                ],
                axis=0,
            )
            more = mm(left[c, i0 : i0 + half, :], b)
            acc = more if acc is None else acc + more
        return acc

    for q, (j0, width) in enumerate(s_.joff):
        st = (sta, stb)[q]
        for i0 in (0, half):
            square = product(i0, j0, width) * scale * scale
            keep = kq[i0 : i0 + half, j0 : j0 + width].astype(F32)
            st[row, i0 : i0 + half, :] = jnp.where(keep > 0.5, square, 0.0).astype(BF)
        start_share(n_piece + q)

    start = (rt[row].astype(F32) * scale).astype(BF)
    moved = 1.5 * mm(fm[...], start)
    out_ref[...] = moved[:, 0 : s_.cols]

    cac[live:, :] = jnp.zeros((wide - live, blk), BF)
    for q, (j0, width) in enumerate(s_.joff):
        st = (sta, stb)[q]
        relay(n_piece + q)
        finish(n_piece + q)
        for r in range(n_row):
            rx[r, :, j0 : j0 + width] = mm(xm[r], st[r]).astype(BF)
        for i0 in (0, half):
            cube = product(i0, j0, width) * scale
            keep = kq[i0 : i0 + half, j0 : j0 + width].astype(F32)
            cac[i0 : i0 + half, j0 : j0 + width] = jnp.where(keep > 0.5, cube, 0.0).astype(BF)
        done = mm(fm[...], cac[:, j0 : j0 + width])
        end = min(j0 + width, s_.cols)
        out_ref[:, j0:end] -= 0.5 * done[:, 0 : end - j0]

    for k in range(1, n_row):
        x_copy(k).wait_send()
        t_copy(k).wait_send()
    for k in range(1, n_col):
        p_copy(k).wait_send()
    for p in range(n_piece):

        def sent(q, _):
            c = q * 2 + lo

            @pl.when((q <= hi) & (hi + 1 < outer))
            def _():
                hop(c, p, 0).wait_send()

            @pl.when((q >= hi) & (hi > 0))
            def _():
                hop(c, p, 1).wait_send()

            @pl.when((q == hi) | jnp.logical_not(by_line(hi, q, p)))
            def _():
                hop(c, p, 2).wait_send()

            return 0

        lax.fori_loop(0, outer, sent, 0)
        c_other = hi * 2 + 1 - lo

        @pl.when((hi + 1 < outer) & by_line(hi + 1, hi, p))
        def _():
            hop(c_other, p, 0).wait_send()

        @pl.when((hi > 0) & by_line(hi - 1, hi, p))
        def _():
            hop(c_other, p, 1).wait_send()

    for ix in range(n_piece + 2):
        first, onward = share(ix)
        for cp in first + onward:
            cp.wait_send()


def on_device(hamiltonian, new_atom, pattern):
    rows, cols = hamiltonian.shape
    n_row, n_col = lax.axis_size("row"), lax.axis_size("col")
    ar, ac = pattern.shape
    s = Plan(n_row, n_col, rows, cols, ar, ac)
    vm = pl.BlockSpec(memory_space=pltpu.VMEM)
    dma = pltpu.SemaphoreType.DMA
    n_piece = len(s.sizes)
    slots = n_col * s.slot
    return pl.pallas_call(
        functools.partial(kernel, s, float(rows * n_row)),
        out_shape=jax.ShapeDtypeStruct((rows, cols), F32),
        in_specs=[pl.BlockSpec(memory_space=pl.ANY), vm, vm],
        out_specs=vm,
        scratch_shapes=[
            pltpu.VMEM((rows, cols), BF),
            pltpu.VMEM((s.wide, s.blk), BF),
            pltpu.VMEM((n_row - 1, s.sl, s.blk), BF),
            pltpu.VMEM((n_row - 1, s.slp, s.blk), BF),
            pltpu.VMEM((LANE, LANE), BF),
            pltpu.VMEM((n_col, s.av, LANE), BF),
            pltpu.VMEM((s.live, s.w), BF),
            pltpu.VMEM((s.live, s.blk), BF),
            pltpu.VMEM((n_col, s.live, s.blk), BF),
            pltpu.VMEM((n_col, s.live, slots), BF),
            pltpu.VMEM((s.live, s.blk), F32),
            pltpu.VMEM((n_row, s.wide, s.blk), BF),
            pltpu.VMEM((n_row, s.ratio * slots, s.blk), BF),
            pltpu.VMEM((n_row, s.ratio * slots, s.wide), BF),
            pltpu.VMEM((rows, s.wide), BF),
            pltpu.VMEM((n_row, s.wide, s.joff[0][1]), BF),
            pltpu.VMEM((n_row, s.wide, s.joff[1][1]), BF),
            pltpu.VMEM((s.wide, s.blk), BF),
            pltpu.VMEM((8, s.blk), F32),
            pltpu.VMEM((n_row, 8, LANE), F32),
            dma((1,)),
            dma((n_row,)),
            dma((n_row,)),
            dma((n_col,)),
            dma((n_col,)),
            dma((n_row,)),
            dma((n_row,)),
            dma((3, n_col, n_piece)),
            dma((n_col, n_piece)),
            dma((n_piece + 2, n_row)),
            dma((n_piece + 2, n_row)),
            dma((n_piece + 2, n_row)),
        ],
        compiler_params=pltpu.CompilerParams(
            collective_id=0, has_side_effects=True, vmem_limit_bytes=62 * 1024 * 1024
        ),
    )(hamiltonian, new_atom.reshape(1, -1), pattern)


def solution(mesh):
    in_specs = (P("row", "col"), P(), P("row", "col"))
    out_specs = P("row", "col")
    return jax.shard_map(
        on_device, mesh=mesh, in_specs=in_specs, out_specs=out_specs, check_vma=False
    )
```

time: 121 us -> 115 us (0.950)
  other arithmetic: 5.2 us -> 0 us
  local copies, waits for them, and re-layouts: 7.49 us -> 3.72 us
  Pallas kernels: 108 us -> 110 us
    unnamed x2, local copies, waits for them, and re-layouts: 0.01 us -> 3.72 us
    reshape x4 -> x0, local copies, waits for them, and re-layouts: 2.73 us -> none  [the longest x1 1.1 us: on_device(): return out[:, :cols_here, :cols_here].reshape(rows_here, cols_here)]
    pallas_call x1, Pallas kernels: 108 us -> 110 us  [on_device(): pl.pallas_call(functools.partial(kernel, s, float(rows * n_row)), out_sha...]
    convert_element_type x2 -> x0, other arithmetic: 1.56 us -> none  [the longest x1 0.79 us: on_device(): selrow = ((by_row[:, :, None] == row_here * ar + i) & (i < ar)).astype(BF)]
    pad x4 -> x0, local copies, waits for them, and re-layouts: 1.49 us -> none  [the longest x1 0.88 us: on_device(): jnp.pad(hamiltonian.reshape(ratio, cols_here, cols_here), ((0, 0), (0, pa...]
    slice x1 -> x0, local copies, waits for them, and re-layouts: 1.33 us -> none  [on_device(): return out[:, :cols_here, :cols_here].reshape(rows_here, cols_here)]
where the time goes in v1:
time: 115 us; the launch traced here: 114 us
  Pallas kernels  110 us (96%)
  local copies, waits for them, and re-layouts  3.72 us (3%)
    pallas_call x1, Pallas kernels, on_device(): pl.pallas_call(functools.partial(kernel, s, float(rows * n_row)), out_sha...  110 us
    unnamed x2, local copies, waits for them, and re-layouts  3.72 us

profile of v1, /device:TPU:0, one launch (start us, length us, event | category | flops | bytes accessed | tf_op | source)
XLA Modules:
  0.0 113.8 jit_solution(9082637640555312543)
XLA Ops:
  0.0 1.4 %copy.4.pat_ref = s32[56,28]{1,0:T(8,128)} copy(s32[56,28]{0,1:T(8,128)} %param.5) | data formatting | bytes 12544 | tf_op args[2]
  1.4 110.0 %shard_map.37 = f32[728,364]{1,0:T(8,128)} custom-call(bf16[728,364]{1,0:T(8,128)(2,1)} %h_ref.1, s32[1,224]{1,0:T(1,128)} %bitcast.1, s32[56,28]{1,0:T(8,128)} %copy.4.pat_ref), custom_call_target="tpu_custom_call" | custom-call | tf_op jit(solution)/shard_map/pallas_call | solution.py:505
  111.4 2.3 %copy.6 = f32[728,364]{1,0:T(8,128)} copy(f32[728,364]{1,0:T(8,128)} %shard_map.37) | data formatting | bytes 2119936

commit v2 on v1

--- a/solution.py
+++ b/solution.py
@@ -75,15 +75,19 @@
         chip = (pair[0] + min(pair[1], pair[n_row - 1])) * NBF // 16 * 16
         rest = self.live - chip
         last = up(rest // 4, 16)
-        ends = [0, own, chip, self.live - last, self.live]
+        mid = up((rest - last) // 2, 16)
+        ends = [0, own, chip, chip + mid, self.live - last, self.live]
         self.starts, self.sizes = ends[:-1], [b - a for a, b in zip(ends, ends[1:])]
+        self.groups = [[0, 1], [2, 3], [4]]
+        self.spans = [(ends[g[0]], ends[g[-1] + 1]) for g in self.groups]
+        self.stored = n_row * self.ratio * n_col * self.slot * self.wide * 2 <= 8 * 1024 * 1024
         self.joff = [(0, self.blk - LANE), (self.blk - LANE, LANE)]
 
 
 def kernel(
     s_, order, h_ref, na_ref, pat_ref, out_ref,
-    hv, hp, xs, rin, pp, pt_all, mr, kq, panel, left, racc, rt, rx, xm, fm, sta, stb, cac, tot, tot_all,
-    h_sem, x_send, x_recv, p_send, p_recv, t_send, t_recv, g_send, g_recv, r_send, r_recv, f_send,
+    hp, xs, rin, pp, pt_all, mr, kq, panel, left, pos, pull, rt, rx, xm, fm, sta, stb, cac, tot, tot_all,
+    x_send, x_recv, p_send, p_recv, t_send, t_recv, g_send, g_recv, r_send, r_recv, f_send,
 ):
     n_row, n_col, ratio, nx, outer = s_.n_row, s_.n_col, s_.ratio, s_.nx, s_.outer
     ac, ar, av, W, blk, live, wide = s_.ac, s_.ar, s_.av, s_.w, s_.blk, s_.live, s_.wide
@@ -94,10 +98,9 @@
     x, core = row // 2, row % 2
     peer = x * 2 + 1 - core
     n_piece = len(s_.sizes)
+    n_group = len(s_.groups)
     slots = n_col * slot
 
-    h_copy = pltpu.make_async_copy(h_ref, hv, h_sem.at[0])
-    h_copy.start()
     barrier = pltpu.get_barrier_semaphore()
     for k in range(1, n_row):
         pl.semaphore_signal(barrier, inc=1, device_id={"row": (row + k) % n_row, "col": col}, device_id_type=MESH)
@@ -123,7 +126,7 @@
     dr, vr, okr = places(wr)
     atoms = na_ref[...].astype(F32)
     here = (fiota((W, atoms.shape[1]), 1) == dc * ac + vc) & okc
-    nac = jnp.sum(jnp.where(here, atoms, 0.0), axis=1, keepdims=True)
+    nac = jnp.where(okc, jnp.sum(jnp.where(here, atoms, 0.0), axis=1, keepdims=True), -1.0e5)
     nar = jnp.sum(jnp.where(fiota((W, W), 0) == wr, nac, 0.0), axis=0, keepdims=True)
     bc, srcc, homec, grpc = source(nac, dc)
     br, srcr, homer, grpr = source(nar, dr)
@@ -154,18 +157,15 @@
     }
 
     pp[...] = jnp.zeros_like(pp)
-    pp[0:ar, 0:ac] = pat_ref[...].astype(F32).astype(BF)
-    flip = jnp.where(iota((av, LANE), 0) == iota((av, LANE), 1), 1.0, 0.0).astype(BF)
-    pt_all[col] = mm_nt(flip, pp[...]).astype(BF)
+    pp[0:ac, 0:ar] = pat_ref[...].astype(F32)
+    pt_all[col] = pp[...].astype(BF)
     hp[...] = jnp.zeros_like(hp)
     rin[:, sl:, :] = jnp.zeros((n_row - 1, slp - sl, blk), BF)
     rt[:, live:, :] = jnp.zeros((n_row, wide - live, blk), BF)
     sta[:, live:, :] = jnp.zeros((n_row, wide - live, sta.shape[2]), BF)
     stb[:, live:, :] = jnp.zeros((n_row, wide - live, stb.shape[2]), BF)
     tot[...] = jnp.zeros_like(tot)
-    racc[...] = jnp.zeros_like(racc)
-    h_copy.wait()
-    hp[0 : s_.rows, 0 : s_.cols] = hv[...]
+    hp[0 : s_.rows, 0 : s_.cols] = h_ref[...]
 
     def pick(k):
         xs[k - 1] = mm(onehot(sl, out_place, k * slp), hp[...]).astype(BF)
@@ -210,7 +210,7 @@
     def by_line(at, src, p):
         inner = ((at == 1) & (src == 0)) | ((at == outer - 2) & (src == outer - 1))
         edge = ((at == outer - 1) & (src == outer - 2)) | ((at == 0) & (src == 1))
-        return (inner | edge) if p % 2 == 0 else inner
+        return (inner | edge) if p in (0, 2) else inner
 
     def start_own_piece(p):
         @pl.when(hi + 1 < outer)
@@ -246,35 +246,54 @@
         pltpu.make_async_copy(pt_all.at[src], pt_all.at[src], p_recv.at[src]).wait()
     mr[...] = mm_nt(er, pt_all[...].reshape(W, LANE)).astype(BF)
 
-    slot_at = dc * slot + NBF * rank_slot
     mine = okc & (dc == colf)
-
-    def process(c, p):
-        i0, n = s_.starts[p], s_.sizes[p]
-        lo_c = NBF * (nac - c.astype(F32) * ac)
-        t = fiota((W, blk), 1) - lo_c
-        hit = (t >= 0.0) & (t < NBF) & okc
-        keep = mm(mr[i0 : i0 + n, :], jnp.where(hit, 1.0, 0.0).astype(BF))
-        part = jnp.where(keep > 0.5, panel[c, i0 : i0 + n, :].astype(F32), 0.0)
+    coded = jnp.broadcast_to(jnp.where(okc, dc * 8.0 + rank_slot + 1.0, 0.0), (W, LANE)).astype(BF)
+
+    def atom_of(t):
+        return jnp.where(t < s_.cols, whole_part(t, NBF), -1.0e4)
+
+    atom_c, atom_r = atom_of(fiota((blk, 1), 0)), atom_of(fiota((1, blk), 1))
+    within = fiota((blk, 1), 0) - NBF * atom_c
+    my_tile = pl.multiple_of(col * slot // LANE * LANE, LANE)
+    my_lane = (col * slot % LANE).astype(F32)
+    pull_place = expand(mine, NBF * vc, bc * LANE + my_lane + NBF * rank_slot, blk)
+
+    def chunk_tables(c, _):
+        code = mm(jnp.where(nar - (c * ac).astype(F32) == atom_c, 1.0, 0.0).astype(BF), coded) - 1.0
+        far = jnp.floor(code * 0.125)
+        at = far * slot + NBF * (code - 8.0 * far) + within
+        pos[c] = jnp.where(code < 0.0, -1.0, at)
+        rows = pl.ds(pl.multiple_of(c * LANE, LANE), LANE)
+        pull[rows, :] = onehot(LANE, pull_place - (c * LANE).astype(F32))
+        return 0
+
+    lax.fori_loop(0, n_col, chunk_tables, 0)
+
+    def process(c, g):
+        i0, i1 = s_.spans[g]
+        n = i1 - i0
+        hit = jnp.where(nac - c.astype(F32) * ac == atom_r, 1.0, 0.0).astype(BF)
+        keep = mm(mr[i0:i1, :], hit)
+        part = jnp.where(keep > 0.5, panel[c, i0:i1, :].astype(F32), 0.0)
         tot[...] += jnp.sum((part * part).reshape(n // 8, 8, blk), axis=0)
-        part = part.astype(BF)
-        to_slot = jnp.sum(jnp.where(hit, t + (slot_at + 1.0), 0.0), axis=0, keepdims=True) - 1.0
-        to_new = jnp.sum(jnp.where(hit & mine, t + (NBF * vc + 1.0), 0.0), axis=0, keepdims=True) - 1.0
-        left[c, i0 : i0 + n, :] = mm_nt(part, onehot(slots, to_slot)).astype(BF)
-        racc[i0 : i0 + n, :] += mm_nt(part, onehot(blk, to_new))
+        at = pos[c]
+        lane = fiota((blk, LANE), 1)
+        to_slot = jnp.concatenate(
+            [jnp.where(lane + float(q) == at, 1.0, 0.0).astype(BF) for q in range(0, slots, LANE)], axis=1
+        )
+        left[i0:i1, pl.ds(pl.multiple_of(c * slots, slots), slots)] = mm(part.astype(BF), to_slot).astype(BF)
 
     def arrived(c, p):
         pltpu.make_async_copy(piece(c, p), piece(c, p), g_recv.at[c, p]).wait()
 
-    def gather(p):
-        def step(d, _):
-            for way in range(2):
-                src = hi - d if way == 0 else hi + d
-                ok = (d > 0) & (d < outer) & (src >= 0) & (src < outer)
-
-                @pl.when(ok)
-                def _():
-                    c = src * 2 + lo
+    def forward(d, g):
+        for way in range(2):
+            src = hi - d if way == 0 else hi + d
+
+            @pl.when((src >= 0) & (src < outer))
+            def _():
+                c = src * 2 + lo
+                for p in s_.groups[g]:
                     arrived(c, p)
 
                     @pl.when(hi + 1 < outer if way == 0 else hi > 0)
@@ -285,9 +304,10 @@
                     def _():
                         hop(c, p, 2).start()
 
-            @pl.when(d == 1)
-            def _():
-                c = hi * 2 + 1 - lo
+        @pl.when(d == 1)
+        def _():
+            c = hi * 2 + 1 - lo
+            for p in s_.groups[g]:
                 arrived(c, p)
 
                 @pl.when((hi + 1 < outer) & by_line(hi + 1, hi, p))
@@ -298,33 +318,53 @@
                 def _():
                     hop(c, p, 1).start()
 
-            def candidate(k, _):
-                kind, way = k // 2, k % 2
-                dist = d - kind
-                src = hi + (1 - 2 * way) * dist
-                ok = (dist >= 0) & (dist < outer) & (src >= 0) & (src < outer) & ((dist > 0) | (way == 0))
-
-                @pl.when(ok)
+    def work(e, g):
+        def candidate(k, _):
+            kind, way = k // 2, k % 2
+            dist = e - 1 - kind
+            src = hi + (1 - 2 * way) * dist
+            ok = (dist >= 0) & (dist < outer) & (src >= 0) & (src < outer) & ((dist > 0) | (way == 0))
+
+            @pl.when(ok)
+            def _():
+                c = src * 2 + jnp.where(kind == 0, lo, 1 - lo)
+
+                @pl.when((kind == 1) & (dist > 0))
                 def _():
-                    c = src * 2 + jnp.where(kind == 0, lo, 1 - lo)
-
-                    @pl.when((kind == 1) & (dist > 0))
-                    def _():
+                    for p in s_.groups[g]:
                         arrived(c, p)
 
-                    process(c, p)
-
-                return 0
-
-            lax.fori_loop(0, 4, candidate, 0)
+                process(c, g)
+
             return 0
 
-        lax.fori_loop(0, outer + 1, step, 0)
+        lax.fori_loop(0, 4, candidate, 0)
+
+    def gather(g, between):
+        def step(d, _):
+            forward(d, g)
+            for at, extra in between.items():
+                pl.when(d == at)(extra)
+            if g > 0:
+
+                @pl.when(d <= 2)
+                def _():
+                    work(outer - 1 + d, g - 1)
+
+                @pl.when(d == 2)
+                def _():
+                    right_share(g - 1)
+
+            work(d, g)
+            return 0
+
+        lax.fori_loop(1, outer, step, 0)
 
     def part_of(r, ix):
-        if ix < n_piece:
-            return rt.at[r, pl.ds(s_.starts[ix], s_.sizes[ix]), :]
-        return (sta, stb)[ix - n_piece].at[r, pl.ds(0, live), :]
+        if ix < n_group:
+            i0, i1 = s_.spans[ix]
+            return rt.at[r, pl.ds(i0, i1 - i0), :]
+        return (sta, stb)[ix - n_group].at[r, pl.ds(0, live), :]
 
     def share(ix):
         def send(r, to, sem):
@@ -356,34 +396,55 @@
         for k in range(nx):
             got(ix, (x + k) % nx * 2 + 1 - core)
 
-    def right_piece(p):
-        i0, n = s_.starts[p], s_.sizes[p]
-        rt[row, i0 : i0 + n, :] = racc[i0 : i0 + n, :].astype(BF)
-        start_share(p)
-
-    gather(0)
-    for k in range(2, n_row):
-        x_copy(k).wait_recv()
-    for p in range(2, n_piece):
-        assemble(p)
-        start_own_piece(p)
-    right_piece(0)
-    gather(1)
-    right_piece(1)
-    relay(0)
-    for r in range(n_row):
+    def right_share(g):
+        i0, i1 = s_.spans[g]
+        mine_first = jnp.concatenate([left[i0:i1, pl.ds(c * slots + my_tile, LANE)] for c in range(n_col)], axis=1)
+        rt[row, i0:i1, :] = mm(mine_first, pull[...]).astype(BF)
+        start_share(g)
+
+    def later_rows():
+        for k in range(2, n_row):
+            x_copy(k).wait_recv()
+        for p in range(2, n_piece):
+            assemble(p)
+            start_own_piece(p)
+
+    def row_places(r):
         ws = slice(r * ratio * av, (r + 1) * ratio * av)
         at = (dc[ws] - float(r * ratio)) * slots + bc[ws] * slot + NBF * rank_slot[ws]
-        xm[r] = onehot(ratio * slots, expand(okc[ws], NBF * rank_all[ws], at, wide))
-    my_new = NBF * ((dc - rowf * ratio) * ac + vc)
-    fm[...] = onehot(s_.rows, expand(to_me, NBF * rank_all, my_new, wide))
-    t = fiota((W, blk), 1) - NBF * vc
-    kq[...] = mm(mr[...], jnp.where((t >= 0.0) & (t < NBF) & mine, 1.0, 0.0).astype(BF)).astype(BF)
-    gather(2)
-    right_piece(2)
+        return expand(okc[ws], NBF * rank_all[ws], at, wide)
+
+    def row_slots(r, a, b):
+        return xm[r, :, a:b] if s_.stored else onehot(ratio * slots, xm[r, 0:1, a:b])
+
+    def row_blocks(visit):
+        if s_.stored:
+            for r in range(n_row):
+                visit(r)
+        else:
+            lax.fori_loop(0, n_row, lambda r, _: (visit(r), 0)[1], 0)
+
+    def tables():
+        for r in range(n_row):
+            at = row_places(r)
+            xm[r] = onehot(ratio * slots, at) if s_.stored else jnp.broadcast_to(at, (8, wide))
+        my_new = NBF * ((dc - rowf * ratio) * ac + vc)
+        fm[...] = onehot(s_.rows, expand(to_me, NBF * rank_all, my_new, wide))
+        t = fiota((W, blk), 1) - NBF * vc
+        kq[...] = mm(mr[...], jnp.where((t >= 0.0) & (t < NBF) & mine, 1.0, 0.0).astype(BF)).astype(BF)
+
+    gather(0, {2: later_rows})
+    gather(1, {1: tables})
+    gather(2, {1: lambda: relay(0)})
+    last = n_group - 1
+
+    def tail(e, _):
+        work(e, last)
+        return 0
+
+    lax.fori_loop(outer, outer + 2, tail, 0)
+    right_share(last)
     relay(1)
-    gather(3)
-    right_piece(3)
 
     def t_copy(k):
         return pltpu.make_async_remote_copy(
@@ -397,33 +458,43 @@
     tot_all[row] = part_sum
     for k in range(1, n_row):
         t_copy(k).start()
+    finish(0)
+    finish(1)
+    early = s_.spans[2][0] // LANE * LANE
+
+    def spread(r, rows, j0, width, add):
+        for q in range(n_col * ratio):
+            at = pl.ds(r * ratio * slot + q % n_col * slots + q // n_col * slot, slot)
+            if not s_.stored:
+                at = pl.ds(pl.multiple_of(at.start, slot), slot)
+            part = rows[q * slot : (q + 1) * slot].astype(BF)
+            if add:
+                rx[at, j0 : j0 + width] += part
+            else:
+                rx[at, j0 : j0 + width] = part
+
+    row_blocks(lambda r: spread(r, mm(row_slots(r, 0, early), rt[r, 0:early, :]), 0, blk, False))
     relay(2)
-    for p in range(3):
-        finish(p)
-    relay(3)
-    finish(3)
-    for r in range(n_row):
-        rx[r] = mm(xm[r], rt[r]).astype(BF)
+    finish(2)
+    row_blocks(lambda r: spread(r, mm(row_slots(r, early, wide), rt[r, early:, :]), 0, blk, True))
     for k in range(1, n_row):
         src = (row + k) % n_row
         pltpu.make_async_copy(tot_all.at[src], tot_all.at[src], t_recv.at[src]).wait()
     total = jnp.sum(jnp.sum(tot_all[...], axis=0), axis=(0, 1), keepdims=True)
     scale = lax.rsqrt(total / order)
+
     half = live // 2
 
     def product(i0, j0, width):
-        acc = None
-        for c in range(n_col):
-            b = jnp.concatenate(
-                [
-                    rx[d // ratio, (d % ratio) * slots + c * slot : (d % ratio) * slots + (c + 1) * slot, j0 : j0 + width]
-                    for d in range(n_col)
-                ],
-                axis=0,
-            )
-            more = mm(left[c, i0 : i0 + half, :], b)
-            acc = more if acc is None else acc + more
-        return acc
+        depth = min(n_col * slots, 4096)
+        if depth == n_col * slots:
+            return mm(left[i0 : i0 + half, :], rx[:, j0 : j0 + width])
+
+        def more(q, acc):
+            k = pl.ds(pl.multiple_of(q * slots, slots), slots)
+            return acc + mm(left[i0 : i0 + half, k], rx[k, j0 : j0 + width])
+
+        return lax.fori_loop(0, n_col, more, jnp.zeros((half, width), F32))
 
     for q, (j0, width) in enumerate(s_.joff):
         st = (sta, stb)[q]
@@ -431,19 +502,61 @@
             square = product(i0, j0, width) * scale * scale
             keep = kq[i0 : i0 + half, j0 : j0 + width].astype(F32)
             st[row, i0 : i0 + half, :] = jnp.where(keep > 0.5, square, 0.0).astype(BF)
-        start_share(n_piece + q)
+        start_share(n_group + q)
 
     start = (rt[row].astype(F32) * scale).astype(BF)
     moved = 1.5 * mm(fm[...], start)
     out_ref[...] = moved[:, 0 : s_.cols]
 
+    for k in range(1, n_row):
+        x_copy(k).wait_send()
+        t_copy(k).wait_send()
+    for k in range(1, n_col):
+        p_copy(k).wait_send()
+    for p in range(n_piece):
+
+        def sent(q, _):
+            c = q * 2 + lo
+
+            @pl.when((q <= hi) & (hi + 1 < outer))
+            def _():
+                hop(c, p, 0).wait_send()
+
+            @pl.when((q >= hi) & (hi > 0))
+            def _():
+                hop(c, p, 1).wait_send()
+
+            @pl.when((q == hi) | jnp.logical_not(by_line(hi, q, p)))
+            def _():
+                hop(c, p, 2).wait_send()
+
+            return 0
+
+        lax.fori_loop(0, outer, sent, 0)
+        c_other = hi * 2 + 1 - lo
+
+        @pl.when((hi + 1 < outer) & by_line(hi + 1, hi, p))
+        def _():
+            hop(c_other, p, 0).wait_send()
+
+        @pl.when((hi > 0) & by_line(hi - 1, hi, p))
+        def _():
+            hop(c_other, p, 1).wait_send()
+
+    def sent_share(ix):
+        first, onward = share(ix)
+        for cp in first + onward:
+            cp.wait_send()
+
+    for ix in range(n_group):
+        sent_share(ix)
+
     cac[live:, :] = jnp.zeros((wide - live, blk), BF)
     for q, (j0, width) in enumerate(s_.joff):
         st = (sta, stb)[q]
-        relay(n_piece + q)
-        finish(n_piece + q)
-        for r in range(n_row):
-            rx[r, :, j0 : j0 + width] = mm(xm[r], st[r]).astype(BF)
+        relay(n_group + q)
+        finish(n_group + q)
+        row_blocks(lambda r: spread(r, mm(row_slots(r, 0, wide), st[r]), j0, width, False))
         for i0 in (0, half):
             cube = product(i0, j0, width) * scale
             keep = kq[i0 : i0 + half, j0 : j0 + width].astype(F32)
@@ -452,45 +565,8 @@
         end = min(j0 + width, s_.cols)
         out_ref[:, j0:end] -= 0.5 * done[:, 0 : end - j0]
 
-    for k in range(1, n_row):
-        x_copy(k).wait_send()
-        t_copy(k).wait_send()
-    for k in range(1, n_col):
-        p_copy(k).wait_send()
-    for p in range(n_piece):
-
-        def sent(q, _):
-            c = q * 2 + lo
-
-            @pl.when((q <= hi) & (hi + 1 < outer))
-            def _():
-                hop(c, p, 0).wait_send()
-
-            @pl.when((q >= hi) & (hi > 0))
-            def _():
-                hop(c, p, 1).wait_send()
-
-            @pl.when((q == hi) | jnp.logical_not(by_line(hi, q, p)))
-            def _():
-                hop(c, p, 2).wait_send()
-
-            return 0
-
-        lax.fori_loop(0, outer, sent, 0)
-        c_other = hi * 2 + 1 - lo
-
-        @pl.when((hi + 1 < outer) & by_line(hi + 1, hi, p))
-        def _():
-            hop(c_other, p, 0).wait_send()
-
-        @pl.when((hi > 0) & by_line(hi - 1, hi, p))
-        def _():
-            hop(c_other, p, 1).wait_send()
-
-    for ix in range(n_piece + 2):
-        first, onward = share(ix)
-        for cp in first + onward:
-            cp.wait_send()
+    for q in range(2):
+        sent_share(n_group + q)
 
 
 def on_device(hamiltonian, new_atom, pattern):
@@ -501,34 +577,38 @@
     vm = pl.BlockSpec(memory_space=pltpu.VMEM)
     dma = pltpu.SemaphoreType.DMA
     n_piece = len(s.sizes)
+    n_group = len(s.groups)
     slots = n_col * s.slot
+    buffers = [
+        pltpu.VMEM((s.wide, s.blk), BF),
+        pltpu.VMEM((n_row - 1, s.sl, s.blk), BF),
+        pltpu.VMEM((n_row - 1, s.slp, s.blk), BF),
+        pltpu.VMEM((s.av, LANE), F32),
+        pltpu.VMEM((n_col, s.av, LANE), BF),
+        pltpu.VMEM((s.live, s.w), BF),
+        pltpu.VMEM((s.live, s.blk), BF),
+        pltpu.VMEM((n_col, s.live, s.blk), BF),
+        pltpu.VMEM((s.live, n_col * slots), BF),
+        pltpu.VMEM((n_col, s.blk, LANE), F32),
+        pltpu.VMEM((n_col * LANE, s.blk), BF),
+        pltpu.VMEM((n_row, s.wide, s.blk), BF),
+        pltpu.VMEM((n_col * slots, s.blk), BF),
+        pltpu.VMEM((n_row, s.ratio * slots, s.wide) if s.stored else (n_row, 8, s.wide), BF if s.stored else F32),
+        pltpu.VMEM((rows, s.wide), BF),
+        pltpu.VMEM((n_row, s.wide, s.joff[0][1]), BF),
+        pltpu.VMEM((n_row, s.wide, s.joff[1][1]), BF),
+        pltpu.VMEM((s.wide, s.blk), BF),
+        pltpu.VMEM((8, s.blk), F32),
+        pltpu.VMEM((n_row, 8, LANE), F32),
+    ]
+    held = sum(int(np.prod(b.shape)) * np.dtype(b.dtype).itemsize for b in buffers)
     return pl.pallas_call(
         functools.partial(kernel, s, float(rows * n_row)),
         out_shape=jax.ShapeDtypeStruct((rows, cols), F32),
-        in_specs=[pl.BlockSpec(memory_space=pl.ANY), vm, vm],
+        in_specs=[vm, vm, vm],
         out_specs=vm,
         scratch_shapes=[
-            pltpu.VMEM((rows, cols), BF),
-            pltpu.VMEM((s.wide, s.blk), BF),
-            pltpu.VMEM((n_row - 1, s.sl, s.blk), BF),
-            pltpu.VMEM((n_row - 1, s.slp, s.blk), BF),
-            pltpu.VMEM((LANE, LANE), BF),
-            pltpu.VMEM((n_col, s.av, LANE), BF),
-            pltpu.VMEM((s.live, s.w), BF),
-            pltpu.VMEM((s.live, s.blk), BF),
-            pltpu.VMEM((n_col, s.live, s.blk), BF),
-            pltpu.VMEM((n_col, s.live, slots), BF),
-            pltpu.VMEM((s.live, s.blk), F32),
-            pltpu.VMEM((n_row, s.wide, s.blk), BF),
-            pltpu.VMEM((n_row, s.ratio * slots, s.blk), BF),
-            pltpu.VMEM((n_row, s.ratio * slots, s.wide), BF),
-            pltpu.VMEM((rows, s.wide), BF),
-            pltpu.VMEM((n_row, s.wide, s.joff[0][1]), BF),
-            pltpu.VMEM((n_row, s.wide, s.joff[1][1]), BF),
-            pltpu.VMEM((s.wide, s.blk), BF),
-            pltpu.VMEM((8, s.blk), F32),
-            pltpu.VMEM((n_row, 8, LANE), F32),
-            dma((1,)),
+            *buffers,
             dma((n_row,)),
             dma((n_row,)),
             dma((n_col,)),
@@ -537,14 +617,14 @@
             dma((n_row,)),
             dma((3, n_col, n_piece)),
             dma((n_col, n_piece)),
-            dma((n_piece + 2, n_row)),
-            dma((n_piece + 2, n_row)),
-            dma((n_piece + 2, n_row)),
+            dma((n_group + 2, n_row)),
+            dma((n_group + 2, n_row)),
+            dma((n_group + 2, n_row)),
         ],
         compiler_params=pltpu.CompilerParams(
-            collective_id=0, has_side_effects=True, vmem_limit_bytes=62 * 1024 * 1024
+            collective_id=0, has_side_effects=True, vmem_limit_bytes=min(held + held // 8 + 7 * 1024 * 1024, 62 * 1024 * 1024)
         ),
-    )(hamiltonian, new_atom.reshape(1, -1), pattern)
+    )(hamiltonian, new_atom.reshape(1, -1), pattern.T)
 
 
 def solution(mesh):

time: 115 us -> 95.7 us (0.83)
  Pallas kernels: 110 us -> 91.9 us
    pallas_call x1, Pallas kernels: 110 us -> 91.9 us  [on_device(): pl.pallas_call(functools.partial(kernel, s, float(rows * n_row)), out_sha...]
    unnamed x2 -> x7, local copies, waits for them, and re-layouts: 3.72 us -> 3.44 us
where the time goes in v2:
time: 95.7 us; the launch traced here: 95.4 us
  Pallas kernels  91.9 us (96%)
  local copies, waits for them, and re-layouts  3.44 us (4%)
    pallas_call x1, Pallas kernels, on_device(): pl.pallas_call(functools.partial(kernel, s, float(rows * n_row)), out_sha...  91.9 us
    unnamed x7, local copies, waits for them, and re-layouts  3.44 us

profile of v2, /device:TPU:0, one launch (start us, length us, event | category | flops | bytes accessed | tf_op | source)
XLA Modules:
  0.0 95.4 jit_solution(15155522252212699945)
XLA Ops:
  0.0 0.0 copy-start
  0.0 1.1 %copy-done = bf16[728,364]{1,0:T(8,128)(2,1)S(1)} copy-done((bf16[728,364]{1,0:T(8,128)(2,1)S(1)}, bf16[728,364]{1,0:T(8,128)(2,1)}, u32[]{:S(2)}) %copy-start) | copy-done | bytes 530008
  1.1 0.0 copy-start.1
  1.1 0.7 copy-done.1
  1.8 0.0 copy-start.2
  1.8 0.7 copy-done.2
  2.5 91.9 %shard_map.37 = f32[728,364]{1,0:T(8,128)S(1)} custom-call(bf16[728,364]{1,0:T(8,128)(2,1)S(1)} %copy-done, s32[1,224]{1,0:T(1,128)S(1)} %bitcast.3, s32[28,56]{1,0:T(8,128)S(1)} %bitcast.2), custom_call_target="tpu_custom_call" | custom-call | tf_op jit(solution)/shard_map/pallas_call | solution.py:605
  94.4 1.0 %copy.5 = f32[728,364]{1,0:T(8,128)} copy(f32[728,364]{1,0:T(8,128)S(1)} %shard_map.37) | data formatting | bytes 2119936
Async XLA Ops:
  0.0 1.1 %copy-start = (bf16[728,364]{1,0:T(8,128)(2,1)S(1)}, bf16[728,364]{1,0:T(8,128)(2,1)}, u32[]{:S(2)}) copy-start(bf16[728,364]{1,0:T(8,128)(2,1)} %h_ref.1) | copy-start | bytes 1589956
  1.1 0.7 copy-start.1
  1.8 0.7 copy-start.2

commit v3 on v2

--- a/solution.py
+++ b/solution.py
@@ -74,7 +74,7 @@
         own = pair[0] * NBF // 16 * 16
         chip = (pair[0] + min(pair[1], pair[n_row - 1])) * NBF // 16 * 16
         rest = self.live - chip
-        last = up(rest // 4, 16)
+        last = up(rest // 3, 16)
         mid = up((rest - last) // 2, 16)
         ends = [0, own, chip, chip + mid, self.live - last, self.live]
         self.starts, self.sizes = ends[:-1], [b - a for a, b in zip(ends, ends[1:])]
@@ -231,20 +231,9 @@
         pick(k)
         x_copy(k).start()
 
-    er_at = fiota((1, LANE), 1)
-    er_d = whole_part(er_at, ac)
-    er_w = (rowf * ratio + er_d) * av + er_at - er_d * ac
-    first = jnp.sum(jnp.where((wc == er_w) & (er_at < ar), NBF * rank_all + 1.0e6, 0.0), axis=0, keepdims=True) - 1.0e6
-    u = fiota((live, LANE), 0) - first
-    er = jnp.where((u >= 0.0) & (u < NBF), 1.0, 0.0).astype(BF)
-
     x_copy(1).wait_recv()
     assemble(1)
     start_own_piece(1)
-    for k in range(1, n_col):
-        src = (col + k) % n_col
-        pltpu.make_async_copy(pt_all.at[src], pt_all.at[src], p_recv.at[src]).wait()
-    mr[...] = mm_nt(er, pt_all[...].reshape(W, LANE)).astype(BF)
 
     mine = okc & (dc == colf)
     coded = jnp.broadcast_to(jnp.where(okc, dc * 8.0 + rank_slot + 1.0, 0.0), (W, LANE)).astype(BF)
@@ -267,7 +256,20 @@
         pull[rows, :] = onehot(LANE, pull_place - (c * LANE).astype(F32))
         return 0
 
-    lax.fori_loop(0, n_col, chunk_tables, 0)
+    def masks_and_tables():
+        er_at = fiota((1, LANE), 1)
+        er_d = whole_part(er_at, ac)
+        er_w = (rowf * ratio + er_d) * av + er_at - er_d * ac
+        first = jnp.sum(jnp.where((wc == er_w) & (er_at < ar), NBF * rank_all + 1.0e6, 0.0), axis=0, keepdims=True) - 1.0e6
+        u = fiota((live, LANE), 0) - first
+        er = jnp.where((u >= 0.0) & (u < NBF), 1.0, 0.0).astype(BF)
+
+        for k in range(1, n_col):
+            src = (col + k) % n_col
+            pltpu.make_async_copy(pt_all.at[src], pt_all.at[src], p_recv.at[src]).wait()
+        mr[...] = mm_nt(er, pt_all[...].reshape(W, LANE)).astype(BF)
+        lax.fori_loop(0, n_col, chunk_tables, 0)
+
 
     def process(c, g):
         i0, i1 = s_.spans[g]
@@ -287,13 +289,13 @@
         pltpu.make_async_copy(piece(c, p), piece(c, p), g_recv.at[c, p]).wait()
 
     def forward(d, g):
-        for way in range(2):
-            src = hi - d if way == 0 else hi + d
-
-            @pl.when((src >= 0) & (src < outer))
-            def _():
-                c = src * 2 + lo
-                for p in s_.groups[g]:
+        for p in s_.groups[g]:
+            for way in range(2):
+                src = hi - d if way == 0 else hi + d
+
+                @pl.when((src >= 0) & (src < outer))
+                def _():
+                    c = src * 2 + lo
                     arrived(c, p)
 
                     @pl.when(hi + 1 < outer if way == 0 else hi > 0)
@@ -304,10 +306,9 @@
                     def _():
                         hop(c, p, 2).start()
 
-        @pl.when(d == 1)
-        def _():
-            c = hi * 2 + 1 - lo
-            for p in s_.groups[g]:
+            @pl.when(d == 1)
+            def _():
+                c = hi * 2 + 1 - lo
                 arrived(c, p)
 
                 @pl.when((hi + 1 < outer) & by_line(hi + 1, hi, p))
@@ -433,7 +434,7 @@
         t = fiota((W, blk), 1) - NBF * vc
         kq[...] = mm(mr[...], jnp.where((t >= 0.0) & (t < NBF) & mine, 1.0, 0.0).astype(BF)).astype(BF)
 
-    gather(0, {2: later_rows})
+    gather(0, {1: masks_and_tables, 2: later_rows})
     gather(1, {1: tables})
     gather(2, {1: lambda: relay(0)})
     last = n_group - 1
@@ -554,13 +555,16 @@
     cac[live:, :] = jnp.zeros((wide - live, blk), BF)
     for q, (j0, width) in enumerate(s_.joff):
         st = (sta, stb)[q]
-        relay(n_group + q)
+        if q == 0:
+            relay(n_group)
         finish(n_group + q)
         row_blocks(lambda r: spread(r, mm(row_slots(r, 0, wide), st[r]), j0, width, False))
         for i0 in (0, half):
             cube = product(i0, j0, width) * scale
             keep = kq[i0 : i0 + half, j0 : j0 + width].astype(F32)
             cac[i0 : i0 + half, j0 : j0 + width] = jnp.where(keep > 0.5, cube, 0.0).astype(BF)
+        if q == 0:
+            relay(n_group + 1)
         done = mm(fm[...], cac[:, j0 : j0 + width])
         end = min(j0 + width, s_.cols)
         out_ref[:, j0:end] -= 0.5 * done[:, 0 : end - j0]

time: 95.7 us -> 91.4 us (0.955)
  Pallas kernels: 91.9 us -> 87.7 us
    pallas_call x1, Pallas kernels: 91.9 us -> 87.7 us  [on_device(): pl.pallas_call(functools.partial(kernel, s, float(rows * n_row)), out_sha...]
where the time goes in v3:
time: 91.4 us; the launch traced here: 91.1 us
  Pallas kernels  87.7 us (96%)
  local copies, waits for them, and re-layouts  3.44 us (4%)
    pallas_call x1, Pallas kernels, on_device(): pl.pallas_call(functools.partial(kernel, s, float(rows * n_row)), out_sha...  87.7 us
    unnamed x7, local copies, waits for them, and re-layouts  3.44 us

profile of v3, /device:TPU:0, one launch (start us, length us, event | category | flops | bytes accessed | tf_op | source)
XLA Modules:
  0.0 91.1 jit_solution(10911247939441965571)
XLA Ops:
  0.0 0.0 copy-start
  0.0 1.1 %copy-done = bf16[728,364]{1,0:T(8,128)(2,1)S(1)} copy-done((bf16[728,364]{1,0:T(8,128)(2,1)S(1)}, bf16[728,364]{1,0:T(8,128)(2,1)}, u32[]{:S(2)}) %copy-start) | copy-done | bytes 530008
  1.1 0.0 copy-start.1
  1.1 0.7 copy-done.1
  1.8 0.0 copy-start.2
  1.8 0.7 copy-done.2
  2.5 87.7 %shard_map.37 = f32[728,364]{1,0:T(8,128)S(1)} custom-call(bf16[728,364]{1,0:T(8,128)(2,1)S(1)} %copy-done, s32[1,224]{1,0:T(1,128)S(1)} %bitcast.3, s32[28,56]{1,0:T(8,128)S(1)} %bitcast.2), custom_call_target="tpu_custom_call" | custom-call | tf_op jit(solution)/shard_map/pallas_call | solution.py:609
  90.1 1.0 %copy.5 = f32[728,364]{1,0:T(8,128)} copy(f32[728,364]{1,0:T(8,128)S(1)} %shard_map.37) | data formatting | bytes 2119936
Async XLA Ops:
  0.0 1.1 %copy-start = (bf16[728,364]{1,0:T(8,128)(2,1)S(1)}, bf16[728,364]{1,0:T(8,128)(2,1)}, u32[]{:S(2)}) copy-start(bf16[728,364]{1,0:T(8,128)(2,1)} %h_ref.1) | copy-start | bytes 1589956
  1.1 0.7 copy-start.1
  1.8 0.7 copy-start.2

commit v4 on v3

--- a/solution.py
+++ b/solution.py
@@ -184,6 +184,7 @@
                 part = more if part is None else part + more
         panel[col, i0 : i0 + n, :] = part.astype(BF)
 
+    assemble(0)
     pl.semaphore_wait(barrier, n_row + n_col - 2)
 
     def x_copy(k):
@@ -223,10 +224,9 @@
 
         hop(col, p, 2).start()
 
+    start_own_piece(0)
     for k in range(1, n_col):
         p_copy(k).start()
-    assemble(0)
-    start_own_piece(0)
     for k in [*range(2, n_row), 1]:
         pick(k)
         x_copy(k).start()

time: 91.4 us -> 91.4 us (level)
  no operation moved by 1% of the time
where the time goes in v4:
time: 91.4 us; the launch traced here: 91.1 us
  Pallas kernels  87.7 us (96%)
  local copies, waits for them, and re-layouts  3.44 us (4%)
    pallas_call x1, Pallas kernels, on_device(): pl.pallas_call(functools.partial(kernel, s, float(rows * n_row)), out_sha...  87.7 us
    unnamed x7, local copies, waits for them, and re-layouts  3.44 us

profile of v4, /device:TPU:0, one launch (start us, length us, event | category | flops | bytes accessed | tf_op | source)
XLA Modules:
  0.0 91.1 jit_solution(13602266550522876989)
XLA Ops:
  0.0 0.0 copy-start
  0.0 1.1 %copy-done = bf16[728,364]{1,0:T(8,128)(2,1)S(1)} copy-done((bf16[728,364]{1,0:T(8,128)(2,1)S(1)}, bf16[728,364]{1,0:T(8,128)(2,1)}, u32[]{:S(2)}) %copy-start) | copy-done | bytes 530008
  1.1 0.0 copy-start.1
  1.1 0.7 copy-done.1
  1.8 0.0 copy-start.2
  1.8 0.7 copy-done.2
  2.5 87.7 %shard_map.37 = f32[728,364]{1,0:T(8,128)S(1)} custom-call(bf16[728,364]{1,0:T(8,128)(2,1)S(1)} %copy-done, s32[1,224]{1,0:T(1,128)S(1)} %bitcast.3, s32[28,56]{1,0:T(8,128)S(1)} %bitcast.2), custom_call_target="tpu_custom_call" | custom-call | tf_op jit(solution)/shard_map/pallas_call | solution.py:609
  90.1 1.0 %copy.5 = f32[728,364]{1,0:T(8,128)} copy(f32[728,364]{1,0:T(8,128)S(1)} %shard_map.37) | data formatting | bytes 2119936
Async XLA Ops:
  0.0 1.1 %copy-start = (bf16[728,364]{1,0:T(8,128)(2,1)S(1)}, bf16[728,364]{1,0:T(8,128)(2,1)}, u32[]{:S(2)}) copy-start(bf16[728,364]{1,0:T(8,128)(2,1)} %h_ref.1) | copy-start | bytes 1589956
  1.1 0.7 copy-start.1
  1.8 0.7 copy-start.2
